TPU v7x, 512 devices: a whole 4x8x8 slice. The times are simulated.
512 devices in a mesh: sub: 16 (over z, core), blk: 32 (over x, y).
Axes of the slice: x: 4, y: 8, z: 8, core: 2. Of those that a mesh axis runs over, the one named last changes fastest.
Arguments:
- double_layer: bfloat16 [16, 2, 2048, 2048], P('sub', None, 'blk'), may hold values from -1 to 2
- single_layer: bfloat16 [16, 2, 2048, 2048], P('sub', None, 'blk'), may hold values from -1 to 2
- hypersingular: bfloat16 [16, 2, 2048, 2048], P('sub', None, 'blk'), may hold values from -1 to 2
- adjoint_double: bfloat16 [16, 2, 2048, 2048], P('sub', None, 'blk'), may hold values from -1 to 2
- matching: int32 [16, 1024], replicated, may hold values from 0 to 1023, each once within a row
- right_side: float32 [16, 2, 2, 2048, 64], P('sub', None, None, 'blk'), may hold values from -6 to 6
- start: float32 [16, 2, 2, 2048, 64], P('sub', None, None, 'blk'), may hold values from -4 to 4
Outputs:
- solution: float32 [16, 2, 2, 2048, 64], P('sub', None, None, 'blk')
Inputs may be any that keep to these rules, and one draw needn't show every extreme that they name: `matching`: each row is a permutation of 0 to 1023; row 0 pairs with no subdomain below and is not read.
All inputs are finite; a program needn't handle non-finite values.
Results may differ from a plain program's by a relative error of at most 0.015.
Values may be sent and summed in bfloat16 or wider, within the bound.
No kernel may reach another device: no remote copies, remote signals or barrier semaphores. Data moves between devices by JAX's collectives and lax.ppermute only.
A program may use at most 64 MiB of HBM per device.

v0:
```python
import jax
import jax.numpy as jnp
from jax import lax
from jax.sharding import Mesh
from jax.sharding import PartitionSpec as P

BASIS = 5
SUB = ("sub_0", "sub_1")
BLK = ("blk_0", "blk_1")


EPSILON = 1e-06


def passed_along(block, axis, distance):
    devices = range(lax.axis_size(axis))
    route = [(i - distance, i) for i in devices if i - distance in devices]
    return lax.ppermute(block, axis, route)


def copy_for_each(value, axis):
    peers = lax.axis_size(axis)
    return lax.all_to_all(
        jnp.broadcast_to(value[None], (peers, *value.shape)), axis, 0, 0, tiled=True
    )


def summed_over(value, axis):
    return jnp.sum(copy_for_each(value, axis), axis=0)


def padded_rows(value, multiple):
    missing = -value.shape[0] % multiple
    return jnp.pad(value, ((0, missing), (0, 0)))


def folded(dots):
    width = dots.shape[1] // 2
    return dots[:, :width] + dots[:, width:]


def summed_everywhere(dots):
    count = dots.shape[0]
    rows = folded(padded_rows(dots, 16))
    half = rows.shape[0] // 2
    packed = jnp.concatenate([rows[:half], rows[half:]], axis=1)
    packed = summed_over(summed_over(packed, SUB), BLK)
    width = rows.shape[1]
    return jnp.concatenate([packed[:, :width], packed[:, width:]])[:count]


def inward(field):
    local_field = field[0]
    return jnp.concatenate([local_field[:, 0], local_field[:, 1]], axis=-1)


def outward(vector):
    width = vector.shape[-1] // 2
    return jnp.stack([vector[..., :width], vector[..., width:]], axis=1)[None]


def tile_of_operators(double_layer, single_layer, hypersingular, adjoint_double):
    columns = lax.axis_size("blk_0")
    grid = ((-double_layer, single_layer), (hypersingular, adjoint_double))
    traces = []
    for line in grid:
        pieces = []
        for part in range(2):
            for operator in line:
                rows, full = operator[part].shape
                pieces.append(
                    jnp.moveaxis(operator[part].reshape(rows, columns, full // columns), 1, 0)
                )
        traces.append(jnp.concatenate(pieces, axis=-1))
    strips = jnp.concatenate(traces, axis=1)
    blocks = lax.all_to_all(strips, "blk_0", 0, 0, tiled=True)
    return blocks.reshape(-1, blocks.shape[-1])


def selectors(matching, local_rows):
    subdomains = lax.axis_size(SUB)
    lines = lax.axis_size("blk_0")
    own_index = lax.axis_index(SUB)
    above_index = jnp.minimum(own_index + 1, subdomains - 1)
    perm_here = lax.dynamic_index_in_dim(matching, own_index, 0, keepdims=False)
    perm_above = lax.dynamic_index_in_dim(matching, above_index, 0, keepdims=False)
    half_rows = local_rows // 2
    half = perm_here.shape[0]
    spots = jnp.arange(half, dtype=jnp.int32)

    def window(values):
        table = values.reshape(lines, lax.axis_size("blk_1"), half_rows)
        return lax.dynamic_index_in_dim(
            table, lax.axis_index("blk_1"), 1, keepdims=False
        ).reshape(-1)

    wanted = window(spots)
    inverse_here = jnp.sum(
        jnp.where(perm_here[None, :] == wanted[:, None], spots[None, :], 0), axis=1
    )
    dofs = jnp.concatenate([2 * window(perm_above) + 1, 2 * inverse_here])
    width = 2 * half // lines
    columns = lax.axis_index("blk_0") * width + jnp.arange(width, dtype=jnp.int32)
    return (dofs[:, None] == columns[None, :]).astype(jnp.bfloat16)


def side_by_side(blocks):
    count, rows, width = blocks.shape
    return jnp.moveaxis(blocks.reshape(count, 2, rows // 2, width), 0, 1).reshape(
        2, count * rows // 2, width
    )


def partial_products(tile, columns):
    width = columns.shape[-1] // 2
    turned = jnp.concatenate([-columns[..., width:], columns[..., :width]], axis=-1)
    stacked = jnp.stack([columns, turned]).reshape(tile.shape[1], 2 * width)
    products = jnp.dot(tile, stacked, preferred_element_type=jnp.float32)
    return products.reshape(lax.axis_size("blk_0"), -1, 2 * width)


def coupling_partials(selector, columns):
    lines = lax.axis_size("blk_0")
    chosen = jnp.einsum(
        "sk,tkn->tsn", selector, columns, preferred_element_type=jnp.float32
    ).astype(jnp.bfloat16)
    middle = chosen.shape[1] // 2
    lower_face = passed_along(chosen[:, :middle], SUB, 1)
    upper_face = passed_along(chosen[:, middle:], SUB, -1)
    joined = jnp.stack([lower_face, upper_face], axis=2)
    joined = joined.reshape(2, lines, 2 * middle // lines, chosen.shape[-1])
    signs = jnp.array([1.0, -1.0], jnp.float32).reshape(1, 2, 1, 1)
    signed = jnp.moveaxis(joined, 1, 0).astype(jnp.float32) * signs
    return signed.reshape(lines, -1, signed.shape[-1])


def exchanged_rows(partials):
    return lax.all_to_all(partials, "blk_0", 0, 0, tiled=True).astype(jnp.float32)


def reduced_rows(partials):
    return jnp.sum(exchanged_rows(partials.astype(jnp.bfloat16)), axis=0)


def in_three_pieces(value):
    high = lax.reduce_precision(value, 8, 7)
    middle = lax.reduce_precision(value - high, 8, 7)
    low = lax.reduce_precision(value - high - middle, 8, 7)
    return jnp.concatenate([high, middle, low]).astype(jnp.bfloat16)


def sum_of_pieces(blocks, lines):
    carried = blocks[:, : 3 * lines].astype(jnp.float32)
    return jnp.sum(carried.reshape(-1, 3, lines, carried.shape[-1]), axis=(0, 1))


def preconditioned(tile, selector, vector, dots=None):
    shape = vector.shape
    width = shape[-1]
    payload = vector.astype(jnp.bfloat16).reshape(-1, width)
    rows = payload.shape[0]
    if dots is not None:
        payload, dots = lax.optimization_barrier((payload, dots))
    blocks = copy_for_each(payload, "blk_1")
    if dots is not None:
        blocks, dots = lax.optimization_barrier((blocks, dots))
        dots = summed_over(padded_rows(dots, 8), SUB)[: dots.shape[0]]
    columns = side_by_side(blocks)
    products = lax.optimization_barrier(partial_products(tile, columns))
    first = products - 0.5 * coupling_partials(selector, columns)
    first = first.astype(jnp.bfloat16)
    if dots is None:
        middle = reduced_rows(first).astype(jnp.bfloat16)
        middle_columns = side_by_side(copy_for_each(middle, "blk_1"))
        return reduced_rows(partial_products(tile, middle_columns)).reshape(shape)
    lines = dots.shape[0]
    pieces = padded_rows(in_three_pieces(dots), 16)
    first, pieces = lax.optimization_barrier((first, pieces))
    middle = reduced_rows(first).astype(jnp.bfloat16)
    blocks = copy_for_each(jnp.concatenate([middle, pieces]), "blk_1")
    second = partial_products(tile, side_by_side(blocks[:, :rows])).astype(jnp.bfloat16)
    carried = in_three_pieces(sum_of_pieces(blocks[:, rows:], lines))
    carried = padded_rows(carried, 16)
    carried = jnp.broadcast_to(carried[None], (second.shape[0], *carried.shape))
    exchanged = exchanged_rows(jnp.concatenate([second, carried], axis=1))
    image = jnp.sum(exchanged[:, :rows], axis=0).reshape(shape)
    return image, folded(sum_of_pieces(exchanged[:, rows:], lines))


def inner_local(first, second):
    return jnp.sum(first * second, axis=(0, 1))


def spread(values):
    return jnp.concatenate([values, values])


def least_squares(hessen, beta):
    gram = [
        [sum(a * b for a, b in zip(hessen[row], hessen[column])) for column in range(row + 1)]
        for row in range(BASIS)
    ]
    factor = [[None] * BASIS for _ in range(BASIS)]
    inverse = [None] * BASIS
    for row in range(BASIS):
        for column in range(row):
            rest = gram[row][column]
            for k in range(column):
                rest = rest - factor[row][k] * factor[column][k]
            factor[row][column] = rest * inverse[column]
        rest = gram[row][row]
        for k in range(row):
            rest = rest - factor[row][k] * factor[row][k]
        factor[row][row] = jnp.sqrt(rest)
        inverse[row] = 1.0 / factor[row][row]
    forward = []
    for row in range(BASIS):
        rest = beta * hessen[row][0]
        for k in range(row):
            rest = rest - factor[row][k] * forward[k]
        forward.append(rest * inverse[row])
    weights = [None] * BASIS
    for row in reversed(range(BASIS)):
        rest = forward[row]
        for k in range(row + 1, BASIS):
            rest = rest - factor[k][row] * weights[k]
        weights[row] = rest * inverse[row]
    return weights


def product_of(first, second, gram):
    total = 0.0
    for i, left in first.items():
        total = total + left * sum(gram[i][k] * right for k, right in second.items())
    return total


def combined(terms):
    total = {}
    for factor, coordinates in terms:
        for i, value in coordinates.items():
            total[i] = total[i] + factor * value if i in total else factor * value
    return total


def arnoldi_step(vectors, image, gram):
    column = [product_of(vector, image, gram) for vector in vectors]
    rest = combined([(1.0, image)] + [(-h, v) for h, v in zip(column, vectors)])
    height = jnp.sqrt(jnp.maximum(product_of(rest, rest, gram), 0.0) + EPSILON)
    inverse = 1.0 / height
    return column, height, {i: value * inverse for i, value in rest.items()}


def spanned(coordinates, vectors):
    total = 0.0
    for i, value in coordinates.items():
        factor = value if isinstance(value, float) else spread(value)
        total = total + factor * vectors[i]
    return total


def completed(known, values, size):
    values = list(values)
    table = [[None] * size for _ in range(size)]
    for i in range(size):
        for k in range(i + 1):
            entry = known[i][k] if i < len(known) else values.pop(0)
            table[i][k] = table[k][i] = entry
    return table


def rows_of_products(vectors, known):
    return [
        inner_local(vectors[i], vectors[k]) for i in range(known, len(vectors)) for k in range(i + 1)
    ]


def body(double_layer, single_layer, hypersingular, adjoint_double, matching, right_side, start):
    tile = tile_of_operators(
        double_layer[0], single_layer[0], hypersingular[0], adjoint_double[0]
    )
    start_local = inward(start)
    selector = selectors(matching, start_local.shape[1])
    start_image = preconditioned(tile, selector, start_local)
    start_image, start, right_side = lax.optimization_barrier((start_image, start, right_side))
    start_again = inward(start)
    residual = inward(right_side) - start_image
    dots = jnp.stack(
        [
            inner_local(residual, residual),
            inner_local(start_again, start_image),
            inner_local(start_again, start_again),
        ]
    )
    applied, sums = preconditioned(tile, selector, residual, dots)
    beta = jnp.sqrt(sums[0] + EPSILON)
    shift = sums[1] / (sums[2] + EPSILON)
    inverse = spread(1.0 / beta)
    basis = [residual * inverse]
    image = applied * inverse
    gram = [[sums[0] / (beta * beta)]]

    wide = spread(shift)
    first = image - wide * basis[0]
    first, basis, gram, shift, wide, beta = lax.optimization_barrier(
        (first, basis, gram, shift, wide, beta)
    )
    first_image = preconditioned(tile, selector, first)
    first_image, first, basis = lax.optimization_barrier((first_image, first, basis))
    second = first_image - wide * first
    spanning = basis + [first, second]
    dots = jnp.stack(rows_of_products(spanning, 1))
    second_image, sums = preconditioned(tile, selector, second, dots)
    second_image, sums, spanning, gram, shift = lax.optimization_barrier(
        (second_image, sums, spanning, gram, shift)
    )
    table = completed(gram, sums, 3)
    vectors = [{0: 1.0}]
    images = [{0: shift, 1: 1.0}, {1: shift, 2: 1.0}]
    column, height, following = arnoldi_step(vectors, images[0], table)
    hessen = [column + [height]]
    vectors.append(following)
    image_ahead = combined([(value, images[i]) for i, value in following.items()])
    column, height, following = arnoldi_step(vectors, image_ahead, table)
    hessen.append(column + [height])
    vectors.append(following)
    image = spanned(following, [spanned(known, spanning) for known in images] + [second_image])
    basis = [spanned(vector, spanning) for vector in vectors]
    gram = [
        [product_of(vectors[i], vectors[k], table) for k in range(i + 1)] for i in range(3)
    ]

    shift = hessen[1][1]
    growth = jnp.sqrt(sum(value * value for value in hessen[1]))
    wide, narrower = spread(shift), spread(1.0 / growth)
    third = image - wide * basis[2]
    third, basis, hessen, gram, shift, growth, wide, narrower, beta, start_again = (
        lax.optimization_barrier(
            (third, basis, hessen, gram, shift, growth, wide, narrower, beta, start_again)
        )
    )
    third_image = preconditioned(tile, selector, third)
    third_image, third, wide, narrower = lax.optimization_barrier(
        (third_image, third, wide, narrower)
    )
    fourth = (third_image - wide * third) * narrower
    fourth, wide, narrower = lax.optimization_barrier((fourth, wide, narrower))
    fourth_image = preconditioned(tile, selector, fourth)
    fourth_image, fourth, third, basis, wide, narrower = lax.optimization_barrier(
        (fourth_image, fourth, third, basis, wide, narrower)
    )
    fifth = (fourth_image - wide * fourth) * narrower
    spanning = basis + [third, fourth, fifth]
    dots = jnp.stack(rows_of_products(spanning, 3))
    dots, spanning, hessen, gram, shift, growth, beta, start_again = lax.optimization_barrier(
        (dots, spanning, hessen, gram, shift, growth, beta, start_again)
    )
    sums = summed_everywhere(dots)
    sums, spanning, hessen, gram, shift, growth, beta, start_again = lax.optimization_barrier(
        (sums, spanning, hessen, gram, shift, growth, beta, start_again)
    )
    table = completed(gram, sums, 6)
    images = [
        dict(enumerate(hessen[0])),
        dict(enumerate(hessen[1])),
        {2: shift, 3: 1.0},
        {3: shift, 4: growth},
        {4: shift, 5: growth},
    ]
    vectors = [{i: 1.0} for i in range(3)]
    while len(hessen) < BASIS:
        image_ahead = combined([(value, images[i]) for i, value in vectors[-1].items()])
        column, height, following = arnoldi_step(vectors, image_ahead, table)
        hessen.append(column + [height])
        if len(hessen) < BASIS:
            vectors.append(following)
    hessen = [list(column) + [jnp.zeros_like(beta)] * (BASIS + 1 - len(column)) for column in hessen]
    weights = least_squares(hessen, beta)
    mixture = combined(list(zip(weights, vectors)))
    solution = start_again + spanned(mixture, spanning)
    return outward(solution)


def solution(mesh):
    torus = Mesh(mesh.devices.reshape(8, 2, 4, 8), ("sub_0", "sub_1", "blk_0", "blk_1"))
    placed = (
        P(SUB, None, BLK, None),
        P(SUB, None, BLK, None),
        P(SUB, None, BLK, None),
        P(SUB, None, BLK, None),
        P(),
        P(SUB, None, None, BLK, None),
        P(SUB, None, None, BLK, None),
    )
    return jax.shard_map(
        body, mesh=torus, in_specs=placed, out_specs=P(SUB, None, None, BLK, None), check_vma=False
    )
```

profile of v0, /device:TPU:1, one launch (start us, length us, event | category | flops | bytes accessed | tf_op | source)
XLA Modules:
  0.0 402.3 jit_solution(17421143999462176974)
XLA Ops:
  0.0 1.0 convert_bitcast_fusion
  1.8 7.6 %all-to-all-start.1 = ((bf16[8,128,128]{2,1,0:T(8,128)(2,1)}), bf16[8,128,128]{2,1,0:T(8,128)(2,1)S(1)}, u32[]{:S(2)}, u32[]{:S(2)}) async-start(bf16[8,128,128]{2,1,0:T(8,128)(2,1)} %broadcast_in_dim.56), calls=%async_computation.1 | async-start | bytes 524288 | tf_op jit(solution)/shard_map/all_to_all | solution.py:23
  9.5 1.1 fusion.230
  14.1 1.5 maximum_maximum_fusion
  15.7 3.3 all-to-all-done.1
  18.9 5.1 %all-to-all-start = ((bf16[4,128,2048]{2,1,0:T(8,128)(2,1)}), bf16[4,128,2048]{2,1,0:T(8,128)(2,1)S(1)}, u32[]{:S(2)}, u32[]{:S(2)}) async-start(bf16[4,128,2048]{2,1,0:T(8,128)(2,1)} %maximum_maximum_fusion), calls=%async_computation | async-start | bytes 4194304 | tf_op jit(solution)/shard_map/all_to_all | solution.py:76
  24.6 4.5 %collective-permute-start.1 = (bf16[2,128,128]{1,2,0:T(8,128)(2,1)S(1)}, bf16[2,128,128]{1,2,0:T(8,128)(2,1)S(1)}, u32[]{:S(2)}, u32[]{:S(2)}) collective-permute-start(bf16[2,128,128]{1,2,0:T(8,128)(2,1)S(1)} %get-tuple-element.372), channel_id=1, source_target_pairs={{32,0},{64,32},{96,64},{128,96},{160,128},{192,160},{224,192},{256... | collective-permute-start | bytes 196616 | tf_op jit(solution)/shard_map/ppermute | solution.py:18
  29.2 3.9 collective-permute-start
  34.7 13.1 %all-to-all-done = bf16[4,128,2048]{2,1,0:T(8,128)(2,1)S(1)} async-done(((bf16[4,128,2048]{2,1,0:T(8,128)(2,1)}), bf16[4,128,2048]{2,1,0:T(8,128)(2,1)S(1)}, u32[]{:S(2)}, u32[]{:S(2)}) %all-to-all-start) | async-done | bytes 2097184 | tf_op jit(solution)/shard_map/all_to_all | solution.py:76
  48.6 7.2 %all_to_all.145 = bf16[4,128,128]{2,1,0:T(8,128)(2,1)S(1)} all-to-all(bf16[4,128,128]{2,1,0:T(8,128)(2,1)S(1)} %fusion.33), channel_id=1, replica_groups=mesh['sub_0'=8,'sub_1'=2,'blk_0'=4,'blk_1'=8] {'blk_0'}, dimensions={0} | all-to-all | bytes 262144 | tf_op jit(solution)/shard_map/all_to_all | solution.py:138
  55.8 13.1 %all_to_all.146 = bf16[8,128,128]{2,1,0:T(8,128)(2,1)S(1)} all-to-all(bf16[8,128,128]{2,1,0:T(8,128)(2,1)S(1)} %broadcast_in_dim.59), channel_id=1, replica_groups=mesh['sub_0'=8,'sub_1'=2,'blk_0'=4,'blk_1'=8] {'blk_1'}, dimensions={0} | all-to-all | bytes 524288 | tf_op jit(solution)/shard_map/all_to_all | solution.py:23
  70.1 7.2 %all_to_all.147 = bf16[4,128,128]{2,1,0:T(8,128)(2,1)S(1)} all-to-all(bf16[4,128,128]{2,1,0:T(8,128)(2,1)S(1)} %convolution_convert_fusion.10), channel_id=1, replica_groups=mesh['sub_0'=8,'sub_1'=2,'blk_0'=4,'blk_1'=8] {'blk_0'}, dimensions={0} | all-to-all | bytes 262144 | tf_op jit(solution)/shard_map/all_to_all | solution.py:138
  77.6 11.7 %all_to_all.148 = bf16[8,128,128]{2,1,0:T(8,128)(2,1)S(1)} all-to-all(bf16[8,128,128]{2,1,0:T(8,128)(2,1)S(1)} %broadcast_in_dim.60), channel_id=1, replica_groups=mesh['sub_0'=8,'sub_1'=2,'blk_0'=4,'blk_1'=8] {'blk_1'}, dimensions={0} | all-to-all | bytes 524288 | tf_op jit(solution)/shard_map/all_to_all | solution.py:23
  89.9 9.0 %collective-permute-start.3 = (bf16[2,128,128]{1,2,0:T(8,128)(2,1)S(1)}, bf16[2,128,128]{1,2,0:T(8,128)(2,1)S(1)}, u32[]{:S(2)}, u32[]{:S(2)}) collective-permute-start(bf16[2,128,128]{1,2,0:T(8,128)(2,1)S(1)} %get-tuple-element.366), channel_id=1, source_target_pairs={{32,0},{64,32},{96,64},{128,96},{160,128},{192,160},{224,192},{256... | collective-permute-start | bytes 196616 | tf_op jit(solution)/shard_map/ppermute | solution.py:18
  98.9 3.9 collective-permute-start.2
  104.4 9.5 %all-to-all-start.6 = ((f32[16,8,128]{2,1,0:T(8,128)}), f32[16,8,128]{2,1,0:T(8,128)S(1)}, u32[]{:S(2)}, u32[]{:S(2)}) async-start(f32[16,8,128]{2,1,0:T(8,128)} %broadcast_in_dim.61), calls=%async_computation.6 | async-start | bytes 131072 | tf_op jit(solution)/shard_map/all_to_all | solution.py:23
  114.3 7.4 %all-to-all-done.6 = f32[16,8,128]{2,1,0:T(8,128)S(1)} async-done(((f32[16,8,128]{2,1,0:T(8,128)}), f32[16,8,128]{2,1,0:T(8,128)S(1)}, u32[]{:S(2)}, u32[]{:S(2)}) %all-to-all-start.6) | async-done | bytes 65568 | tf_op jit(solution)/shard_map/all_to_all | solution.py:23
  121.7 7.3 %all_to_all.149 = bf16[4,128,128]{2,1,0:T(8,128)(2,1)S(1)} all-to-all(bf16[4,128,128]{2,1,0:T(8,128)(2,1)S(1)} %fusion.30), channel_id=1, replica_groups=mesh['sub_0'=8,'sub_1'=2,'blk_0'=4,'blk_1'=8] {'blk_0'}, dimensions={0} | all-to-all | bytes 262144 | tf_op jit(solution)/shard_map/all_to_all | solution.py:138
  129.1 13.0 %all_to_all.150 = bf16[8,144,128]{2,1,0:T(8,128)(2,1)S(1)} all-to-all(bf16[8,144,128]{2,1,0:T(8,128)(2,1)S(1)} %broadcast_in_dim.62), channel_id=1, replica_groups=mesh['sub_0'=8,'sub_1'=2,'blk_0'=4,'blk_1'=8] {'blk_1'}, dimensions={0} | all-to-all | bytes 589824 | tf_op jit(solution)/shard_map/all_to_all | solution.py:23
  143.4 7.3 %all_to_all.151 = bf16[4,144,128]{2,1,0:T(8,128)(2,1)S(1)} all-to-all(bf16[4,144,128]{2,1,0:T(8,128)(2,1)S(1)} %pad_maximum_fusion.12), channel_id=1, replica_groups=mesh['sub_0'=8,'sub_1'=2,'blk_0'=4,'blk_1'=8] {'blk_0'}, dimensions={0} | all-to-all | bytes 294912 | tf_op jit(solution)/shard_map/all_to_all | solution.py:138
  151.1 12.6 %all_to_all.152 = bf16[8,128,128]{2,1,0:T(8,128)(2,1)S(1)} all-to-all(bf16[8,128,128]{2,1,0:T(8,128)(2,1)S(1)} %broadcast_in_dim.65), channel_id=1, replica_groups=mesh['sub_0'=8,'sub_1'=2,'blk_0'=4,'blk_1'=8] {'blk_1'}, dimensions={0} | all-to-all | bytes 524288 | tf_op jit(solution)/shard_map/all_to_all | solution.py:23
  164.2 6.2 %collective-permute-start.5 = (bf16[2,128,128]{1,2,0:T(8,128)(2,1)S(1)}, bf16[2,128,128]{1,2,0:T(8,128)(2,1)S(1)}, u32[]{:S(2)}, u32[]{:S(2)}) collective-permute-start(bf16[2,128,128]{1,2,0:T(8,128)(2,1)S(1)} %get-tuple-element.364), channel_id=1, source_target_pairs={{32,0},{64,32},{96,64},{128,96},{160,128},{192,160},{224,192},{256... | collective-permute-start | bytes 196616 | tf_op jit(solution)/shard_map/ppermute | solution.py:18
  170.5 1.9 collective-permute-start.4
  174.1 7.3 %all_to_all.153 = bf16[4,128,128]{2,1,0:T(8,128)(2,1)S(1)} all-to-all(bf16[4,128,128]{2,1,0:T(8,128)(2,1)S(1)} %fusion.27), channel_id=1, replica_groups=mesh['sub_0'=8,'sub_1'=2,'blk_0'=4,'blk_1'=8] {'blk_0'}, dimensions={0} | all-to-all | bytes 262144 | tf_op jit(solution)/shard_map/all_to_all | solution.py:138
  181.4 12.8 %all_to_all.154 = bf16[8,128,128]{2,1,0:T(8,128)(2,1)S(1)} all-to-all(bf16[8,128,128]{2,1,0:T(8,128)(2,1)S(1)} %broadcast_in_dim.66), channel_id=1, replica_groups=mesh['sub_0'=8,'sub_1'=2,'blk_0'=4,'blk_1'=8] {'blk_1'}, dimensions={0} | all-to-all | bytes 524288 | tf_op jit(solution)/shard_map/all_to_all | solution.py:23
  195.3 7.2 %all_to_all.155 = bf16[4,128,128]{2,1,0:T(8,128)(2,1)S(1)} all-to-all(bf16[4,128,128]{2,1,0:T(8,128)(2,1)S(1)} %convolution_convert_fusion.6), channel_id=1, replica_groups=mesh['sub_0'=8,'sub_1'=2,'blk_0'=4,'blk_1'=8] {'blk_0'}, dimensions={0} | all-to-all | bytes 262144 | tf_op jit(solution)/shard_map/all_to_all | solution.py:138
  202.7 12.1 %all_to_all.156 = bf16[8,128,128]{2,1,0:T(8,128)(2,1)S(1)} all-to-all(bf16[8,128,128]{2,1,0:T(8,128)(2,1)S(1)} %broadcast_in_dim.67), channel_id=1, replica_groups=mesh['sub_0'=8,'sub_1'=2,'blk_0'=4,'blk_1'=8] {'blk_1'}, dimensions={0} | all-to-all | bytes 524288 | tf_op jit(solution)/shard_map/all_to_all | solution.py:23
  215.3 6.5 %collective-permute-start.7 = (bf16[2,128,128]{1,2,0:T(8,128)(2,1)S(1)}, bf16[2,128,128]{1,2,0:T(8,128)(2,1)S(1)}, u32[]{:S(2)}, u32[]{:S(2)}) collective-permute-start(bf16[2,128,128]{1,2,0:T(8,128)(2,1)S(1)} %get-tuple-element.362), channel_id=1, source_target_pairs={{32,0},{64,32},{96,64},{128,96},{160,128},{192,160},{224,192},{256... | collective-permute-start | bytes 196616 | tf_op jit(solution)/shard_map/ppermute | solution.py:18
  221.8 3.0 collective-permute-start.6
  226.4 3.7 all-to-all-start.15
  230.5 7.4 %all-to-all-done.15 = f32[16,8,128]{2,1,0:T(8,128)S(1)} async-done(((f32[16,8,128]{2,1,0:T(8,128)}), f32[16,8,128]{2,1,0:T(8,128)S(1)}, u32[]{:S(2)}, u32[]{:S(2)}) %all-to-all-start.15) | async-done | bytes 65568 | tf_op jit(solution)/shard_map/all_to_all | solution.py:23
  237.9 7.3 %all_to_all.157 = bf16[4,128,128]{2,1,0:T(8,128)(2,1)S(1)} all-to-all(bf16[4,128,128]{2,1,0:T(8,128)(2,1)S(1)} %fusion.24), channel_id=1, replica_groups=mesh['sub_0'=8,'sub_1'=2,'blk_0'=4,'blk_1'=8] {'blk_0'}, dimensions={0} | all-to-all | bytes 262144 | tf_op jit(solution)/shard_map/all_to_all | solution.py:138
  245.4 13.0 %all_to_all.158 = bf16[8,144,128]{2,1,0:T(8,128)(2,1)S(1)} all-to-all(bf16[8,144,128]{2,1,0:T(8,128)(2,1)S(1)} %broadcast_in_dim.69), channel_id=1, replica_groups=mesh['sub_0'=8,'sub_1'=2,'blk_0'=4,'blk_1'=8] {'blk_1'}, dimensions={0} | all-to-all | bytes 589824 | tf_op jit(solution)/shard_map/all_to_all | solution.py:23
  259.6 7.3 %all_to_all.159 = bf16[4,144,128]{2,1,0:T(8,128)(2,1)S(1)} all-to-all(bf16[4,144,128]{2,1,0:T(8,128)(2,1)S(1)} %pad_maximum_fusion.13), channel_id=1, replica_groups=mesh['sub_0'=8,'sub_1'=2,'blk_0'=4,'blk_1'=8] {'blk_0'}, dimensions={0} | all-to-all | bytes 294912 | tf_op jit(solution)/shard_map/all_to_all | solution.py:138
  267.9 12.6 %all_to_all.160 = bf16[8,128,128]{2,1,0:T(8,128)(2,1)S(1)} all-to-all(bf16[8,128,128]{2,1,0:T(8,128)(2,1)S(1)} %broadcast_in_dim.72), channel_id=1, replica_groups=mesh['sub_0'=8,'sub_1'=2,'blk_0'=4,'blk_1'=8] {'blk_1'}, dimensions={0} | all-to-all | bytes 524288 | tf_op jit(solution)/shard_map/all_to_all | solution.py:23
  281.1 6.2 %collective-permute-start.9 = (bf16[2,128,128]{1,2,0:T(8,128)(2,1)S(1)}, bf16[2,128,128]{1,2,0:T(8,128)(2,1)S(1)}, u32[]{:S(2)}, u32[]{:S(2)}) collective-permute-start(bf16[2,128,128]{1,2,0:T(8,128)(2,1)S(1)} %get-tuple-element.359), channel_id=1, source_target_pairs={{32,0},{64,32},{96,64},{128,96},{160,128},{192,160},{224,192},{256... | collective-permute-start | bytes 196616 | tf_op jit(solution)/shard_map/ppermute | solution.py:18
  287.3 1.9 collective-permute-start.8
  290.9 7.3 %all_to_all.161 = bf16[4,128,128]{2,1,0:T(8,128)(2,1)S(1)} all-to-all(bf16[4,128,128]{2,1,0:T(8,128)(2,1)S(1)} %fusion.21), channel_id=1, replica_groups=mesh['sub_0'=8,'sub_1'=2,'blk_0'=4,'blk_1'=8] {'blk_0'}, dimensions={0} | all-to-all | bytes 262144 | tf_op jit(solution)/shard_map/all_to_all | solution.py:138
  298.2 12.6 %all_to_all.162 = bf16[8,128,128]{2,1,0:T(8,128)(2,1)S(1)} all-to-all(bf16[8,128,128]{2,1,0:T(8,128)(2,1)S(1)} %broadcast_in_dim.73), channel_id=1, replica_groups=mesh['sub_0'=8,'sub_1'=2,'blk_0'=4,'blk_1'=8] {'blk_1'}, dimensions={0} | all-to-all | bytes 524288 | tf_op jit(solution)/shard_map/all_to_all | solution.py:23
  311.9 7.2 %all_to_all.163 = bf16[4,128,128]{2,1,0:T(8,128)(2,1)S(1)} all-to-all(bf16[4,128,128]{2,1,0:T(8,128)(2,1)S(1)} %convolution_convert_fusion.2), channel_id=1, replica_groups=mesh['sub_0'=8,'sub_1'=2,'blk_0'=4,'blk_1'=8] {'blk_0'}, dimensions={0} | all-to-all | bytes 262144 | tf_op jit(solution)/shard_map/all_to_all | solution.py:138
  319.3 12.1 %all_to_all.164 = bf16[8,128,128]{2,1,0:T(8,128)(2,1)S(1)} all-to-all(bf16[8,128,128]{2,1,0:T(8,128)(2,1)S(1)} %broadcast_in_dim.75), channel_id=1, replica_groups=mesh['sub_0'=8,'sub_1'=2,'blk_0'=4,'blk_1'=8] {'blk_1'}, dimensions={0} | all-to-all | bytes 524288 | tf_op jit(solution)/shard_map/all_to_all | solution.py:23
  331.9 6.5 %collective-permute-start.11 = (bf16[2,128,128]{1,2,0:T(8,128)(2,1)S(1)}, bf16[2,128,128]{1,2,0:T(8,128)(2,1)S(1)}, u32[]{:S(2)}, u32[]{:S(2)}) collective-permute-start(bf16[2,128,128]{1,2,0:T(8,128)(2,1)S(1)} %get-tuple-element.357), channel_id=1, source_target_pairs={{32,0},{64,32},{96,64},{128,96},{160,128},{192,160},{224,192},{256... | collective-permute-start | bytes 196616 | tf_op jit(solution)/shard_map/ppermute | solution.py:18
  338.4 3.0 collective-permute-start.10
  343.0 7.5 %all_to_all.165 = bf16[4,128,128]{2,1,0:T(8,128)(2,1)S(1)} all-to-all(bf16[4,128,128]{2,1,0:T(8,128)(2,1)S(1)} %fusion.18), channel_id=1, replica_groups=mesh['sub_0'=8,'sub_1'=2,'blk_0'=4,'blk_1'=8] {'blk_0'}, dimensions={0} | all-to-all | bytes 262144 | tf_op jit(solution)/shard_map/all_to_all | solution.py:138
  350.6 14.8 %all_to_all.166 = bf16[8,128,128]{2,1,0:T(8,128)(2,1)S(1)} all-to-all(bf16[8,128,128]{2,1,0:T(8,128)(2,1)S(1)} %broadcast_in_dim.76), channel_id=1, replica_groups=mesh['sub_0'=8,'sub_1'=2,'blk_0'=4,'blk_1'=8] {'blk_1'}, dimensions={0} | all-to-all | bytes 524288 | tf_op jit(solution)/shard_map/all_to_all | solution.py:23
  366.4 7.2 %all_to_all.167 = bf16[4,128,128]{2,1,0:T(8,128)(2,1)S(1)} all-to-all(bf16[4,128,128]{2,1,0:T(8,128)(2,1)S(1)} %convolution_convert_fusion), channel_id=1, replica_groups=mesh['sub_0'=8,'sub_1'=2,'blk_0'=4,'blk_1'=8] {'blk_0'}, dimensions={0} | all-to-all | bytes 262144 | tf_op jit(solution)/shard_map/all_to_all | solution.py:138
  374.0 14.5 %all_to_all.168 = f32[16,8,128]{2,1,0:T(8,128)S(1)} all-to-all(f32[16,8,128]{2,1,0:T(8,128)S(1)} %broadcast_in_dim.77), channel_id=1, replica_groups=mesh['sub_0'=8,'sub_1'=2,'blk_0'=4,'blk_1'=8] {'sub_0','sub_1'}, dimensions={0} | all-to-all | bytes 131072 | tf_op jit(solution)/shard_map/all_to_all | solution.py:23
  388.6 12.1 %all_to_all.169 = f32[32,8,128]{2,1,0:T(8,128)S(1)} all-to-all(f32[32,8,128]{2,1,0:T(8,128)S(1)} %broadcast_in_dim.78), channel_id=1, replica_groups=mesh['sub_0'=8,'sub_1'=2,'blk_0'=4,'blk_1'=8] {'blk_0','blk_1'}, dimensions={0} | all-to-all | bytes 262144 | tf_op jit(solution)/shard_map/all_to_all | solution.py:23
  (275 shorter events, 29.1 us)
Async XLA Ops:
  0.0 10.8 %copy-start = (bf16[1,2,64,2048]{3,2,1,0:T(8,128)(2,1)S(1)}, bf16[1,2,64,2048]{3,2,1,0:T(8,128)(2,1)}, u32[]{:S(2)}) copy-start(bf16[1,2,64,2048]{3,2,1,0:T(8,128)(2,1)} %param.15) | copy-start | bytes 1572868
  1.8 17.1 %all-to-all-start.1 = ((bf16[8,128,128]{2,1,0:T(8,128)(2,1)}), bf16[8,128,128]{2,1,0:T(8,128)(2,1)S(1)}, u32[]{:S(2)}, u32[]{:S(2)}) async-start(bf16[8,128,128]{2,1,0:T(8,128)(2,1)} %broadcast_in_dim.56), calls=%async_computation.1 | async-start | bytes 524288 | tf_op jit(solution)/shard_map/all_to_all | solution.py:23
  9.5 2.0 copy-start.1
  10.8 1.0 copy-start.2
  18.9 28.9 %all-to-all-start = ((bf16[4,128,2048]{2,1,0:T(8,128)(2,1)}), bf16[4,128,2048]{2,1,0:T(8,128)(2,1)S(1)}, u32[]{:S(2)}, u32[]{:S(2)}) async-start(bf16[4,128,2048]{2,1,0:T(8,128)(2,1)} %maximum_maximum_fusion), calls=%async_computation | async-start | bytes 4194304 | tf_op jit(solution)/shard_map/all_to_all | solution.py:76
  24.6 10.0 %copy-start.5 = (f32[2]{0:T(128)S(1)}, f32[2]{0:T(128)}, u32[]{:S(2)}) copy-start(f32[2]{0:T(128)} %constant.68.clone) | copy-start | bytes 28
  24.6 8.8 %collective-permute-start.1 = (bf16[2,128,128]{1,2,0:T(8,128)(2,1)S(1)}, bf16[2,128,128]{1,2,0:T(8,128)(2,1)S(1)}, u32[]{:S(2)}, u32[]{:S(2)}) collective-permute-start(bf16[2,128,128]{1,2,0:T(8,128)(2,1)S(1)} %get-tuple-element.372), channel_id=1, source_target_pairs={{32,0},{64,32},{96,64},{128,96},{160,128},{192,160},{224,192},{256... | collective-permute-start | bytes 196616 | tf_op jit(solution)/shard_map/ppermute | solution.py:18
  29.2 5.2 %collective-permute-start = (bf16[2,128,128]{1,2,0:T(8,128)(2,1)S(1)}, bf16[2,128,128]{1,2,0:T(8,128)(2,1)S(1)}, u32[]{:S(2)}, u32[]{:S(2)}) collective-permute-start(bf16[2,128,128]{1,2,0:T(8,128)(2,1)S(1)} %get-tuple-element.371), channel_id=1, source_target_pairs={{0,32},{32,64},{64,96},{96,128},{128,160},{160,192},{192,224},{224... | collective-permute-start | bytes 196616 | tf_op jit(solution)/shard_map/ppermute | solution.py:18
  69.3 8.0 %copy-start.3 = (f32[1,2,2,64,64]{4,3,2,1,0:T(8,128)S(1)}, f32[1,2,2,64,64]{4,3,2,1,0:T(8,128)}, u32[]{:S(2)}) copy-start(f32[1,2,2,64,64]{4,3,2,1,0:T(8,128)} %param.19) | copy-start | bytes 196612
  69.3 8.0 %copy-start.4 = (f32[1,2,2,64,64]{4,3,2,1,0:T(8,128)S(1)}, f32[1,2,2,64,64]{4,3,2,1,0:T(8,128)}, u32[]{:S(2)}) copy-start(f32[1,2,2,64,64]{4,3,2,1,0:T(8,128)} %param.18) | copy-start | bytes 196612
  89.9 24.0 %collective-permute-start.3 = (bf16[2,128,128]{1,2,0:T(8,128)(2,1)S(1)}, bf16[2,128,128]{1,2,0:T(8,128)(2,1)S(1)}, u32[]{:S(2)}, u32[]{:S(2)}) collective-permute-start(bf16[2,128,128]{1,2,0:T(8,128)(2,1)S(1)} %get-tuple-element.366), channel_id=1, source_target_pairs={{32,0},{64,32},{96,64},{128,96},{160,128},{192,160},{224,192},{256... | collective-permute-start | bytes 196616 | tf_op jit(solution)/shard_map/ppermute | solution.py:18
  98.9 15.0 %collective-permute-start.2 = (bf16[2,128,128]{1,2,0:T(8,128)(2,1)S(1)}, bf16[2,128,128]{1,2,0:T(8,128)(2,1)S(1)}, u32[]{:S(2)}, u32[]{:S(2)}) collective-permute-start(bf16[2,128,128]{1,2,0:T(8,128)(2,1)S(1)} %get-tuple-element.365), channel_id=1, source_target_pairs={{0,32},{32,64},{64,96},{96,128},{128,160},{160,192},{192,224},{224... | collective-permute-start | bytes 196616 | tf_op jit(solution)/shard_map/ppermute | solution.py:18
  104.4 17.3 %all-to-all-start.6 = ((f32[16,8,128]{2,1,0:T(8,128)}), f32[16,8,128]{2,1,0:T(8,128)S(1)}, u32[]{:S(2)}, u32[]{:S(2)}) async-start(f32[16,8,128]{2,1,0:T(8,128)} %broadcast_in_dim.61), calls=%async_computation.6 | async-start | bytes 131072 | tf_op jit(solution)/shard_map/all_to_all | solution.py:23
  164.2 9.1 %collective-permute-start.5 = (bf16[2,128,128]{1,2,0:T(8,128)(2,1)S(1)}, bf16[2,128,128]{1,2,0:T(8,128)(2,1)S(1)}, u32[]{:S(2)}, u32[]{:S(2)}) collective-permute-start(bf16[2,128,128]{1,2,0:T(8,128)(2,1)S(1)} %get-tuple-element.364), channel_id=1, source_target_pairs={{32,0},{64,32},{96,64},{128,96},{160,128},{192,160},{224,192},{256... | collective-permute-start | bytes 196616 | tf_op jit(solution)/shard_map/ppermute | solution.py:18
  170.5 3.2 collective-permute-start.4
  215.3 14.8 %collective-permute-start.7 = (bf16[2,128,128]{1,2,0:T(8,128)(2,1)S(1)}, bf16[2,128,128]{1,2,0:T(8,128)(2,1)S(1)}, u32[]{:S(2)}, u32[]{:S(2)}) collective-permute-start(bf16[2,128,128]{1,2,0:T(8,128)(2,1)S(1)} %get-tuple-element.362), channel_id=1, source_target_pairs={{32,0},{64,32},{96,64},{128,96},{160,128},{192,160},{224,192},{256... | collective-permute-start | bytes 196616 | tf_op jit(solution)/shard_map/ppermute | solution.py:18
  221.8 8.3 %collective-permute-start.6 = (bf16[2,128,128]{1,2,0:T(8,128)(2,1)S(1)}, bf16[2,128,128]{1,2,0:T(8,128)(2,1)S(1)}, u32[]{:S(2)}, u32[]{:S(2)}) collective-permute-start(bf16[2,128,128]{1,2,0:T(8,128)(2,1)S(1)} %get-tuple-element.361), channel_id=1, source_target_pairs={{0,32},{32,64},{64,96},{96,128},{128,160},{160,192},{192,224},{224... | collective-permute-start | bytes 196616 | tf_op jit(solution)/shard_map/ppermute | solution.py:18
  226.4 11.5 %all-to-all-start.15 = ((f32[16,8,128]{2,1,0:T(8,128)}), f32[16,8,128]{2,1,0:T(8,128)S(1)}, u32[]{:S(2)}, u32[]{:S(2)}) async-start(f32[16,8,128]{2,1,0:T(8,128)} %broadcast_in_dim.68), calls=%async_computation.15 | async-start | bytes 131072 | tf_op jit(solution)/shard_map/all_to_all | solution.py:23
  281.1 9.1 %collective-permute-start.9 = (bf16[2,128,128]{1,2,0:T(8,128)(2,1)S(1)}, bf16[2,128,128]{1,2,0:T(8,128)(2,1)S(1)}, u32[]{:S(2)}, u32[]{:S(2)}) collective-permute-start(bf16[2,128,128]{1,2,0:T(8,128)(2,1)S(1)} %get-tuple-element.359), channel_id=1, source_target_pairs={{32,0},{64,32},{96,64},{128,96},{160,128},{192,160},{224,192},{256... | collective-permute-start | bytes 196616 | tf_op jit(solution)/shard_map/ppermute | solution.py:18
  287.3 3.2 collective-permute-start.8
  331.9 10.4 %collective-permute-start.11 = (bf16[2,128,128]{1,2,0:T(8,128)(2,1)S(1)}, bf16[2,128,128]{1,2,0:T(8,128)(2,1)S(1)}, u32[]{:S(2)}, u32[]{:S(2)}) collective-permute-start(bf16[2,128,128]{1,2,0:T(8,128)(2,1)S(1)} %get-tuple-element.357), channel_id=1, source_target_pairs={{32,0},{64,32},{96,64},{128,96},{160,128},{192,160},{224,192},{256... | collective-permute-start | bytes 196616 | tf_op jit(solution)/shard_map/ppermute | solution.py:18
  338.4 4.3 %collective-permute-start.10 = (bf16[2,128,128]{1,2,0:T(8,128)(2,1)S(1)}, bf16[2,128,128]{1,2,0:T(8,128)(2,1)S(1)}, u32[]{:S(2)}, u32[]{:S(2)}) collective-permute-start(bf16[2,128,128]{1,2,0:T(8,128)(2,1)S(1)} %get-tuple-element.356), channel_id=1, source_target_pairs={{0,32},{32,64},{64,96},{96,128},{128,160},{160,192},{192,224},{224... | collective-permute-start | bytes 196616 | tf_op jit(solution)/shard_map/ppermute | solution.py:18
where the time goes:
time: 404 us; the launch traced here: 402 us
  blocking collectives  254 us (63%)
  starting transfers between devices  82.5 us (20%)
  waiting for transfers between devices  33.3 us (8%)
  other arithmetic  11.4 us (3%)
  matrix products  10.6 us (3%)
  local copies, waits for them, and re-layouts  8.63 us (2%)
    all_to_all x13, blocking collectives, copy_for_each(): lax.all_to_all(jnp.broadcast_to(value[None], (peers, *value.shape)), axis...  167 us
    all_to_all x12, blocking collectives, exchanged_rows(): lax.all_to_all(partials, 'blk_0', 0, 0, tiled=True).astype(jnp.float32)  87.4 us
    ppermute x12, starting transfers between devices, passed_along(): return lax.ppermute(block, axis, route)  56.5 us
    all_to_all x3, starting transfers between devices, copy_for_each(): lax.all_to_all(jnp.broadcast_to(value[None], (peers, *value.shape)), axis...  20.9 us
    all_to_all x3, waiting for transfers between devices, copy_for_each(): lax.all_to_all(jnp.broadcast_to(value[None], (peers, *value.shape)), axis...  18.1 us
    all_to_all x1, waiting for transfers between devices, tile_of_operators(): blocks = lax.all_to_all(strips, 'blk_0', 0, 0, tiled=True)  13.1 us
    dot_general x12, matrix products, partial_products(): products = jnp.dot(tile, stacked, preferred_element_type=jnp.float32)  8.49 us
  transfers between devices with their start and end apart: 16, of which 8 were waited for; matrix products, arithmetic and copies ran while one was open for 3% of the time, Pallas kernels for 0%

commit v1 on v0

--- a/solution.py
+++ b/solution.py
@@ -74,7 +74,9 @@
         traces.append(jnp.concatenate(pieces, axis=-1))
     strips = jnp.concatenate(traces, axis=1)
     blocks = lax.all_to_all(strips, "blk_0", 0, 0, tiled=True)
-    return blocks.reshape(-1, blocks.shape[-1])
+    tile = blocks.reshape(-1, blocks.shape[-1])
+    half = tile.shape[1] // 2
+    return lax.optimization_barrier((tile[:, :half], tile[:, half:]))
 
 
 def selectors(matching, local_rows):
@@ -111,12 +113,25 @@
     )
 
 
+def quarter_turn(width):
+    lanes = jnp.arange(width, dtype=jnp.int32)
+    source, target = lanes[:, None], lanes[None, :]
+    half = width // 2
+    plus = (source + half == target).astype(jnp.bfloat16)
+    minus = (source == target + half).astype(jnp.bfloat16)
+    return plus - minus
+
+
 def partial_products(tile, columns):
-    width = columns.shape[-1] // 2
-    turned = jnp.concatenate([-columns[..., width:], columns[..., :width]], axis=-1)
-    stacked = jnp.stack([columns, turned]).reshape(tile.shape[1], 2 * width)
-    products = jnp.dot(tile, stacked, preferred_element_type=jnp.float32)
-    return products.reshape(lax.axis_size("blk_0"), -1, 2 * width)
+    width = columns.shape[-1]
+    stacked = columns.reshape(-1, width)
+    turned = jnp.dot(
+        stacked, quarter_turn(width), preferred_element_type=jnp.float32
+    ).astype(jnp.bfloat16)
+    real, imaginary = tile
+    products = jnp.dot(real, stacked, preferred_element_type=jnp.float32)
+    products = products + jnp.dot(imaginary, turned, preferred_element_type=jnp.float32)
+    return products.reshape(lax.axis_size("blk_0"), -1, width)
 
 
 def coupling_partials(selector, columns):

time: 404 us -> 433 us (1.072)
  other arithmetic: 11.4 us -> 28.3 us
  local copies, waits for them, and re-layouts: 8.63 us -> 16.9 us
  matrix products: 10.6 us -> 15.5 us
    concatenate x1, other arithmetic: 1.52 us -> 18.6 us  [tile_of_operators(): strips = jnp.concatenate(traces, axis=1)]
    dot_general x12 -> x24, matrix products: 8.49 us -> 13.4 us  [the longest x12 8.17 us: partial_products(): jnp.dot(imaginary, turned, preferred_element_type=jnp.float32)]
  transfers between devices with their start and end apart: 16 -> 16, of which waited for: 8 -> 8; matrix products, arithmetic and copies ran while one was open for 3% -> 8% of each run, Pallas kernels for 0% -> 0%
where the time goes in v1:
time: 433 us; the launch traced here: 431 us
  blocking collectives  257 us (59%)
  starting transfers between devices  81.3 us (19%)
  waiting for transfers between devices  30.3 us (7%)
  other arithmetic  28.3 us (7%)
  local copies, waits for them, and re-layouts  16.9 us (4%)
  matrix products  15.5 us (4%)
    all_to_all x13, blocking collectives, copy_for_each(): lax.all_to_all(jnp.broadcast_to(value[None], (peers, *value.shape)), axis...  170 us
    all_to_all x12, blocking collectives, exchanged_rows(): lax.all_to_all(partials, 'blk_0', 0, 0, tiled=True).astype(jnp.float32)  87.5 us
    ppermute x12, starting transfers between devices, passed_along(): return lax.ppermute(block, axis, route)  56.4 us
    all_to_all x3, starting transfers between devices, copy_for_each(): lax.all_to_all(jnp.broadcast_to(value[None], (peers, *value.shape)), axis...  20.9 us
    concatenate x1, other arithmetic, tile_of_operators(): strips = jnp.concatenate(traces, axis=1)  18.6 us
    all_to_all x3, waiting for transfers between devices, copy_for_each(): lax.all_to_all(jnp.broadcast_to(value[None], (peers, *value.shape)), axis...  14.8 us
    all_to_all x1, waiting for transfers between devices, tile_of_operators(): blocks = lax.all_to_all(strips, 'blk_0', 0, 0, tiled=True)  12.3 us
  transfers between devices with their start and end apart: 16, of which 8 were waited for; matrix products, arithmetic and copies ran while one was open for 8% of the time, Pallas kernels for 0%

profile of v1, /device:TPU:1, one launch (start us, length us, event | category | flops | bytes accessed | tf_op | source)
XLA Modules:
  0.0 430.9 jit_solution(15964485801392596448)
XLA Ops:
  1.8 7.6 %all-to-all-start.1 = ((bf16[8,128,128]{2,1,0:T(8,128)(2,1)}), bf16[8,128,128]{2,1,0:T(8,128)(2,1)}, u32[]{:S(2)}, u32[]{:S(2)}) async-start(bf16[8,128,128]{2,1,0:T(8,128)(2,1)} %broadcast_in_dim.56), calls=%async_computation.1 | async-start | bytes 524288 | tf_op jit(solution)/shard_map/all_to_all | solution.py:23
  14.7 18.6 %maximum_maximum_fusion = bf16[4,128,2048]{2,0,1:T(4,128)(2,1)S(1)} fusion(bf16[4,64,512]{2,0,1:T(4,128)(2,1)S(1)} %bitcast.1161, bf16[4,64,512]{2,0,1:T(4,128)(2,1)S(1)} %bitcast.1164, bf16[4,64,512]{2,0,1:T(4,128)(2,1)S(1)} %bitcast.1165, bf16[4,64,512]{2,0,1:T(4,128)(2,1)S(1)} %bitcast.1166, bf16[4,64,512]{2,0,1:T(4,128)(2,1)S(1)} %bitcast.1170, ...), kind=kLoop, calls=%fused_computation | loop fusion | flops 16777216 | bytes 4194304 | tf_op jit(solution)/shard_map/concatenate | solution.py:75
  33.3 2.5 copy.124
  35.9 4.0 all-to-all-start
  42.6 4.8 %collective-permute-start.1 = (bf16[2,128,128]{1,2,0:T(8,128)(2,1)S(1)}, bf16[2,128,128]{1,2,0:T(8,128)(2,1)S(1)}, u32[]{:S(2)}, u32[]{:S(2)}) collective-permute-start(bf16[2,128,128]{1,2,0:T(8,128)(2,1)S(1)} %get-tuple-element.354), channel_id=1, source_target_pairs={{32,0},{64,32},{96,64},{128,96},{160,128},{192,160},{224,192},{256... | collective-permute-start | bytes 196616 | tf_op jit(solution)/shard_map/ppermute | solution.py:18
  47.4 2.3 collective-permute-start
  51.3 12.3 %all-to-all-done = bf16[4,128,2048]{2,1,0:T(8,128)(2,1)S(1)} async-done(((bf16[4,128,2048]{2,1,0:T(8,128)(2,1)}), bf16[4,128,2048]{2,1,0:T(8,128)(2,1)S(1)}, u32[]{:S(2)}, u32[]{:S(2)}) %all-to-all-start) | async-done | bytes 2097184 | tf_op jit(solution)/shard_map/all_to_all | solution.py:76
  63.6 1.3 copy-done
  64.9 1.7 fusion.332
  67.8 7.2 %all_to_all.145 = bf16[4,128,128]{2,1,0:T(8,128)(2,1)S(1)} all-to-all(bf16[4,128,128]{2,1,0:T(8,128)(2,1)S(1)} %fusion.63), channel_id=1, replica_groups=mesh['sub_0'=8,'sub_1'=2,'blk_0'=4,'blk_1'=8] {'blk_0'}, dimensions={0} | all-to-all | bytes 262144 | tf_op jit(solution)/shard_map/all_to_all | solution.py:153
  75.1 15.6 %all_to_all.146 = bf16[8,128,128]{2,1,0:T(8,128)(2,1)S(1)} all-to-all(bf16[8,128,128]{2,1,0:T(8,128)(2,1)S(1)} %broadcast_in_dim.59), channel_id=1, replica_groups=mesh['sub_0'=8,'sub_1'=2,'blk_0'=4,'blk_1'=8] {'blk_1'}, dimensions={0} | all-to-all | bytes 524288 | tf_op jit(solution)/shard_map/all_to_all | solution.py:23
  91.8 7.2 %all_to_all.147 = bf16[4,128,128]{2,1,0:T(8,128)(2,1)S(1)} all-to-all(bf16[4,128,128]{2,1,0:T(8,128)(2,1)S(1)} %bitcast.1195), channel_id=1, replica_groups=mesh['sub_0'=8,'sub_1'=2,'blk_0'=4,'blk_1'=8] {'blk_0'}, dimensions={0} | all-to-all | bytes 262144 | tf_op jit(solution)/shard_map/all_to_all | solution.py:153
  99.3 11.7 %all_to_all.148 = bf16[8,128,128]{2,1,0:T(8,128)(2,1)S(1)} all-to-all(bf16[8,128,128]{2,1,0:T(8,128)(2,1)S(1)} %broadcast_in_dim.60), channel_id=1, replica_groups=mesh['sub_0'=8,'sub_1'=2,'blk_0'=4,'blk_1'=8] {'blk_1'}, dimensions={0} | all-to-all | bytes 524288 | tf_op jit(solution)/shard_map/all_to_all | solution.py:23
  111.9 10.6 %collective-permute-start.3 = (bf16[2,128,128]{1,2,0:T(8,128)(2,1)S(1)}, bf16[2,128,128]{1,2,0:T(8,128)(2,1)S(1)}, u32[]{:S(2)}, u32[]{:S(2)}) collective-permute-start(bf16[2,128,128]{1,2,0:T(8,128)(2,1)S(1)} %get-tuple-element.348), channel_id=1, source_target_pairs={{32,0},{64,32},{96,64},{128,96},{160,128},{192,160},{224,192},{256... | collective-permute-start | bytes 196616 | tf_op jit(solution)/shard_map/ppermute | solution.py:18
  122.6 3.9 collective-permute-start.2
  127.8 9.5 %all-to-all-start.6 = ((f32[16,8,128]{2,1,0:T(8,128)}), f32[16,8,128]{2,1,0:T(8,128)S(1)}, u32[]{:S(2)}, u32[]{:S(2)}) async-start(f32[16,8,128]{2,1,0:T(8,128)} %broadcast_in_dim.61), calls=%async_computation.6 | async-start | bytes 131072 | tf_op jit(solution)/shard_map/all_to_all | solution.py:23
  137.7 7.4 %all-to-all-done.6 = f32[16,8,128]{2,1,0:T(8,128)S(1)} async-done(((f32[16,8,128]{2,1,0:T(8,128)}), f32[16,8,128]{2,1,0:T(8,128)S(1)}, u32[]{:S(2)}, u32[]{:S(2)}) %all-to-all-start.6) | async-done | bytes 65568 | tf_op jit(solution)/shard_map/all_to_all | solution.py:23
  145.2 7.3 %all_to_all.149 = bf16[4,128,128]{2,1,0:T(8,128)(2,1)S(1)} all-to-all(bf16[4,128,128]{2,1,0:T(8,128)(2,1)S(1)} %fusion.60), channel_id=1, replica_groups=mesh['sub_0'=8,'sub_1'=2,'blk_0'=4,'blk_1'=8] {'blk_0'}, dimensions={0} | all-to-all | bytes 262144 | tf_op jit(solution)/shard_map/all_to_all | solution.py:153
  152.6 13.0 %all_to_all.150 = bf16[8,144,128]{2,1,0:T(8,128)(2,1)S(1)} all-to-all(bf16[8,144,128]{2,1,0:T(8,128)(2,1)S(1)} %broadcast_in_dim.62), channel_id=1, replica_groups=mesh['sub_0'=8,'sub_1'=2,'blk_0'=4,'blk_1'=8] {'blk_1'}, dimensions={0} | all-to-all | bytes 589824 | tf_op jit(solution)/shard_map/all_to_all | solution.py:23
  166.9 7.3 %all_to_all.151 = bf16[4,144,128]{2,1,0:T(8,128)(2,1)S(1)} all-to-all(bf16[4,144,128]{2,1,0:T(8,128)(2,1)S(1)} %pad_maximum_fusion), channel_id=1, replica_groups=mesh['sub_0'=8,'sub_1'=2,'blk_0'=4,'blk_1'=8] {'blk_0'}, dimensions={0} | all-to-all | bytes 294912 | tf_op jit(solution)/shard_map/all_to_all | solution.py:153
  175.2 12.6 %all_to_all.152 = bf16[8,128,128]{2,1,0:T(8,128)(2,1)S(1)} all-to-all(bf16[8,128,128]{2,1,0:T(8,128)(2,1)S(1)} %broadcast_in_dim.65), channel_id=1, replica_groups=mesh['sub_0'=8,'sub_1'=2,'blk_0'=4,'blk_1'=8] {'blk_1'}, dimensions={0} | all-to-all | bytes 524288 | tf_op jit(solution)/shard_map/all_to_all | solution.py:23
  188.6 6.2 %collective-permute-start.5 = (bf16[2,128,128]{1,2,0:T(8,128)(2,1)S(1)}, bf16[2,128,128]{1,2,0:T(8,128)(2,1)S(1)}, u32[]{:S(2)}, u32[]{:S(2)}) collective-permute-start(bf16[2,128,128]{1,2,0:T(8,128)(2,1)S(1)} %get-tuple-element.346), channel_id=1, source_target_pairs={{32,0},{64,32},{96,64},{128,96},{160,128},{192,160},{224,192},{256... | collective-permute-start | bytes 196616 | tf_op jit(solution)/shard_map/ppermute | solution.py:18
  194.9 1.9 collective-permute-start.4
  198.5 7.4 %all_to_all.153 = bf16[4,128,128]{2,1,0:T(8,128)(2,1)S(1)} all-to-all(bf16[4,128,128]{2,1,0:T(8,128)(2,1)S(1)} %fusion.57), channel_id=1, replica_groups=mesh['sub_0'=8,'sub_1'=2,'blk_0'=4,'blk_1'=8] {'blk_0'}, dimensions={0} | all-to-all | bytes 262144 | tf_op jit(solution)/shard_map/all_to_all | solution.py:153
  205.9 12.7 %all_to_all.154 = bf16[8,128,128]{2,1,0:T(8,128)(2,1)S(1)} all-to-all(bf16[8,128,128]{2,1,0:T(8,128)(2,1)S(1)} %broadcast_in_dim.66), channel_id=1, replica_groups=mesh['sub_0'=8,'sub_1'=2,'blk_0'=4,'blk_1'=8] {'blk_1'}, dimensions={0} | all-to-all | bytes 524288 | tf_op jit(solution)/shard_map/all_to_all | solution.py:23
  219.7 7.2 %all_to_all.155 = bf16[4,128,128]{2,1,0:T(8,128)(2,1)S(1)} all-to-all(bf16[4,128,128]{2,1,0:T(8,128)(2,1)S(1)} %bitcast.1196), channel_id=1, replica_groups=mesh['sub_0'=8,'sub_1'=2,'blk_0'=4,'blk_1'=8] {'blk_0'}, dimensions={0} | all-to-all | bytes 262144 | tf_op jit(solution)/shard_map/all_to_all | solution.py:153
  227.1 12.0 %all_to_all.156 = bf16[8,128,128]{2,1,0:T(8,128)(2,1)S(1)} all-to-all(bf16[8,128,128]{2,1,0:T(8,128)(2,1)S(1)} %broadcast_in_dim.67), channel_id=1, replica_groups=mesh['sub_0'=8,'sub_1'=2,'blk_0'=4,'blk_1'=8] {'blk_1'}, dimensions={0} | all-to-all | bytes 524288 | tf_op jit(solution)/shard_map/all_to_all | solution.py:23
  240.0 6.5 %collective-permute-start.7 = (bf16[2,128,128]{1,2,0:T(8,128)(2,1)S(1)}, bf16[2,128,128]{1,2,0:T(8,128)(2,1)S(1)}, u32[]{:S(2)}, u32[]{:S(2)}) collective-permute-start(bf16[2,128,128]{1,2,0:T(8,128)(2,1)S(1)} %get-tuple-element.344), channel_id=1, source_target_pairs={{32,0},{64,32},{96,64},{128,96},{160,128},{192,160},{224,192},{256... | collective-permute-start | bytes 196616 | tf_op jit(solution)/shard_map/ppermute | solution.py:18
  246.5 2.9 collective-permute-start.6
  250.7 3.7 all-to-all-start.15
  254.8 7.4 %all-to-all-done.15 = f32[16,8,128]{2,1,0:T(8,128)S(1)} async-done(((f32[16,8,128]{2,1,0:T(8,128)}), f32[16,8,128]{2,1,0:T(8,128)S(1)}, u32[]{:S(2)}, u32[]{:S(2)}) %all-to-all-start.15) | async-done | bytes 65568 | tf_op jit(solution)/shard_map/all_to_all | solution.py:23
  262.3 7.3 %all_to_all.157 = bf16[4,128,128]{2,1,0:T(8,128)(2,1)S(1)} all-to-all(bf16[4,128,128]{2,1,0:T(8,128)(2,1)S(1)} %fusion.54), channel_id=1, replica_groups=mesh['sub_0'=8,'sub_1'=2,'blk_0'=4,'blk_1'=8] {'blk_0'}, dimensions={0} | all-to-all | bytes 262144 | tf_op jit(solution)/shard_map/all_to_all | solution.py:153
  269.7 13.0 %all_to_all.158 = bf16[8,144,128]{2,1,0:T(8,128)(2,1)S(1)} all-to-all(bf16[8,144,128]{2,1,0:T(8,128)(2,1)S(1)} %broadcast_in_dim.69), channel_id=1, replica_groups=mesh['sub_0'=8,'sub_1'=2,'blk_0'=4,'blk_1'=8] {'blk_1'}, dimensions={0} | all-to-all | bytes 589824 | tf_op jit(solution)/shard_map/all_to_all | solution.py:23
  284.0 7.3 %all_to_all.159 = bf16[4,144,128]{2,1,0:T(8,128)(2,1)S(1)} all-to-all(bf16[4,144,128]{2,1,0:T(8,128)(2,1)S(1)} %pad_maximum_fusion.1), channel_id=1, replica_groups=mesh['sub_0'=8,'sub_1'=2,'blk_0'=4,'blk_1'=8] {'blk_0'}, dimensions={0} | all-to-all | bytes 294912 | tf_op jit(solution)/shard_map/all_to_all | solution.py:153
  294.8 12.6 %all_to_all.160 = bf16[8,128,128]{2,1,0:T(8,128)(2,1)S(1)} all-to-all(bf16[8,128,128]{2,1,0:T(8,128)(2,1)S(1)} %broadcast_in_dim.72), channel_id=1, replica_groups=mesh['sub_0'=8,'sub_1'=2,'blk_0'=4,'blk_1'=8] {'blk_1'}, dimensions={0} | all-to-all | bytes 524288 | tf_op jit(solution)/shard_map/all_to_all | solution.py:23
  308.3 6.2 %collective-permute-start.9 = (bf16[2,128,128]{1,2,0:T(8,128)(2,1)S(1)}, bf16[2,128,128]{1,2,0:T(8,128)(2,1)S(1)}, u32[]{:S(2)}, u32[]{:S(2)}) collective-permute-start(bf16[2,128,128]{1,2,0:T(8,128)(2,1)S(1)} %get-tuple-element.341), channel_id=1, source_target_pairs={{32,0},{64,32},{96,64},{128,96},{160,128},{192,160},{224,192},{256... | collective-permute-start | bytes 196616 | tf_op jit(solution)/shard_map/ppermute | solution.py:18
  314.5 1.9 collective-permute-start.8
  318.1 7.4 %all_to_all.161 = bf16[4,128,128]{2,1,0:T(8,128)(2,1)S(1)} all-to-all(bf16[4,128,128]{2,1,0:T(8,128)(2,1)S(1)} %fusion.51), channel_id=1, replica_groups=mesh['sub_0'=8,'sub_1'=2,'blk_0'=4,'blk_1'=8] {'blk_0'}, dimensions={0} | all-to-all | bytes 262144 | tf_op jit(solution)/shard_map/all_to_all | solution.py:153
  325.6 12.7 %all_to_all.162 = bf16[8,128,128]{2,1,0:T(8,128)(2,1)S(1)} all-to-all(bf16[8,128,128]{2,1,0:T(8,128)(2,1)S(1)} %broadcast_in_dim.73), channel_id=1, replica_groups=mesh['sub_0'=8,'sub_1'=2,'blk_0'=4,'blk_1'=8] {'blk_1'}, dimensions={0} | all-to-all | bytes 524288 | tf_op jit(solution)/shard_map/all_to_all | solution.py:23
  339.4 7.2 %all_to_all.163 = bf16[4,128,128]{2,1,0:T(8,128)(2,1)S(1)} all-to-all(bf16[4,128,128]{2,1,0:T(8,128)(2,1)S(1)} %bitcast.1197), channel_id=1, replica_groups=mesh['sub_0'=8,'sub_1'=2,'blk_0'=4,'blk_1'=8] {'blk_0'}, dimensions={0} | all-to-all | bytes 262144 | tf_op jit(solution)/shard_map/all_to_all | solution.py:153
  346.8 12.3 %all_to_all.164 = bf16[8,128,128]{2,1,0:T(8,128)(2,1)S(1)} all-to-all(bf16[8,128,128]{2,1,0:T(8,128)(2,1)S(1)} %broadcast_in_dim.75), channel_id=1, replica_groups=mesh['sub_0'=8,'sub_1'=2,'blk_0'=4,'blk_1'=8] {'blk_1'}, dimensions={0} | all-to-all | bytes 524288 | tf_op jit(solution)/shard_map/all_to_all | solution.py:23
  359.9 6.2 %collective-permute-start.11 = (bf16[2,128,128]{1,2,0:T(8,128)(2,1)S(1)}, bf16[2,128,128]{1,2,0:T(8,128)(2,1)S(1)}, u32[]{:S(2)}, u32[]{:S(2)}) collective-permute-start(bf16[2,128,128]{1,2,0:T(8,128)(2,1)S(1)} %get-tuple-element.339), channel_id=1, source_target_pairs={{32,0},{64,32},{96,64},{128,96},{160,128},{192,160},{224,192},{256... | collective-permute-start | bytes 196616 | tf_op jit(solution)/shard_map/ppermute | solution.py:18
  366.1 2.9 collective-permute-start.10
  371.3 7.5 %all_to_all.165 = bf16[4,128,128]{2,1,0:T(8,128)(2,1)S(1)} all-to-all(bf16[4,128,128]{2,1,0:T(8,128)(2,1)S(1)} %fusion.48), channel_id=1, replica_groups=mesh['sub_0'=8,'sub_1'=2,'blk_0'=4,'blk_1'=8] {'blk_0'}, dimensions={0} | all-to-all | bytes 262144 | tf_op jit(solution)/shard_map/all_to_all | solution.py:153
  378.8 14.8 %all_to_all.166 = bf16[8,128,128]{2,1,0:T(8,128)(2,1)S(1)} all-to-all(bf16[8,128,128]{2,1,0:T(8,128)(2,1)S(1)} %broadcast_in_dim.76), channel_id=1, replica_groups=mesh['sub_0'=8,'sub_1'=2,'blk_0'=4,'blk_1'=8] {'blk_1'}, dimensions={0} | all-to-all | bytes 524288 | tf_op jit(solution)/shard_map/all_to_all | solution.py:23
  394.9 7.2 %all_to_all.167 = bf16[4,128,128]{2,1,0:T(8,128)(2,1)S(1)} all-to-all(bf16[4,128,128]{2,1,0:T(8,128)(2,1)S(1)} %bitcast.1194), channel_id=1, replica_groups=mesh['sub_0'=8,'sub_1'=2,'blk_0'=4,'blk_1'=8] {'blk_0'}, dimensions={0} | all-to-all | bytes 262144 | tf_op jit(solution)/shard_map/all_to_all | solution.py:153
  402.5 14.5 %all_to_all.168 = f32[16,8,128]{2,1,0:T(8,128)S(1)} all-to-all(f32[16,8,128]{2,1,0:T(8,128)S(1)} %broadcast_in_dim.77), channel_id=1, replica_groups=mesh['sub_0'=8,'sub_1'=2,'blk_0'=4,'blk_1'=8] {'sub_0','sub_1'}, dimensions={0} | all-to-all | bytes 131072 | tf_op jit(solution)/shard_map/all_to_all | solution.py:23
  417.0 12.1 %all_to_all.169 = f32[32,8,128]{2,1,0:T(8,128)S(1)} all-to-all(f32[32,8,128]{2,1,0:T(8,128)S(1)} %broadcast_in_dim.78), channel_id=1, replica_groups=mesh['sub_0'=8,'sub_1'=2,'blk_0'=4,'blk_1'=8] {'blk_0','blk_1'}, dimensions={0} | all-to-all | bytes 262144 | tf_op jit(solution)/shard_map/all_to_all | solution.py:23
  (281 shorter events, 39.7 us)
Async XLA Ops:
  0.0 10.8 %copy-start.1 = (bf16[1,2,64,2048]{3,2,1,0:T(8,128)(2,1)S(1)}, bf16[1,2,64,2048]{3,2,1,0:T(8,128)(2,1)}, u32[]{:S(2)}) copy-start(bf16[1,2,64,2048]{3,2,1,0:T(8,128)(2,1)} %param.15) | copy-start | bytes 1572868
  1.8 34.1 %all-to-all-start.1 = ((bf16[8,128,128]{2,1,0:T(8,128)(2,1)}), bf16[8,128,128]{2,1,0:T(8,128)(2,1)}, u32[]{:S(2)}, u32[]{:S(2)}) async-start(bf16[8,128,128]{2,1,0:T(8,128)(2,1)} %broadcast_in_dim.56), calls=%async_computation.1 | async-start | bytes 524288 | tf_op jit(solution)/shard_map/all_to_all | solution.py:23
  9.5 2.0 copy-start.2
  10.8 1.0 copy-start.3
  35.9 27.6 %all-to-all-start = ((bf16[4,128,2048]{2,1,0:T(8,128)(2,1)}), bf16[4,128,2048]{2,1,0:T(8,128)(2,1)S(1)}, u32[]{:S(2)}, u32[]{:S(2)}) async-start(bf16[4,128,2048]{2,1,0:T(8,128)(2,1)} %copy.124), calls=%async_computation | async-start | bytes 4194304 | tf_op jit(solution)/shard_map/all_to_all | solution.py:76
  40.0 11.2 %copy-start.8 = (f32[2]{0:T(128)S(1)}, f32[2]{0:T(128)}, u32[]{:S(2)}) copy-start(f32[2]{0:T(128)} %constant.71.clone) | copy-start | bytes 28
  42.6 7.4 %collective-permute-start.1 = (bf16[2,128,128]{1,2,0:T(8,128)(2,1)S(1)}, bf16[2,128,128]{1,2,0:T(8,128)(2,1)S(1)}, u32[]{:S(2)}, u32[]{:S(2)}) collective-permute-start(bf16[2,128,128]{1,2,0:T(8,128)(2,1)S(1)} %get-tuple-element.354), channel_id=1, source_target_pairs={{32,0},{64,32},{96,64},{128,96},{160,128},{192,160},{224,192},{256... | collective-permute-start | bytes 196616 | tf_op jit(solution)/shard_map/ppermute | solution.py:18
  47.4 3.6 collective-permute-start
  63.6 1.4 copy-start
  90.7 8.4 %copy-start.4 = (f32[1,2,2,64,64]{4,3,2,1,0:T(8,128)S(1)}, f32[1,2,2,64,64]{4,3,2,1,0:T(8,128)}, u32[]{:S(2)}) copy-start(f32[1,2,2,64,64]{4,3,2,1,0:T(8,128)} %param.19) | copy-start | bytes 196612
  90.7 8.4 %copy-start.5 = (f32[1,2,2,64,64]{4,3,2,1,0:T(8,128)S(1)}, f32[1,2,2,64,64]{4,3,2,1,0:T(8,128)}, u32[]{:S(2)}) copy-start(f32[1,2,2,64,64]{4,3,2,1,0:T(8,128)} %param.18) | copy-start | bytes 196612
  111.9 25.4 %collective-permute-start.3 = (bf16[2,128,128]{1,2,0:T(8,128)(2,1)S(1)}, bf16[2,128,128]{1,2,0:T(8,128)(2,1)S(1)}, u32[]{:S(2)}, u32[]{:S(2)}) collective-permute-start(bf16[2,128,128]{1,2,0:T(8,128)(2,1)S(1)} %get-tuple-element.348), channel_id=1, source_target_pairs={{32,0},{64,32},{96,64},{128,96},{160,128},{192,160},{224,192},{256... | collective-permute-start | bytes 196616 | tf_op jit(solution)/shard_map/ppermute | solution.py:18
  122.6 14.8 %collective-permute-start.2 = (bf16[2,128,128]{1,2,0:T(8,128)(2,1)S(1)}, bf16[2,128,128]{1,2,0:T(8,128)(2,1)S(1)}, u32[]{:S(2)}, u32[]{:S(2)}) collective-permute-start(bf16[2,128,128]{1,2,0:T(8,128)(2,1)S(1)} %get-tuple-element.347), channel_id=1, source_target_pairs={{0,32},{32,64},{64,96},{96,128},{128,160},{160,192},{192,224},{224... | collective-permute-start | bytes 196616 | tf_op jit(solution)/shard_map/ppermute | solution.py:18
  127.8 17.3 %all-to-all-start.6 = ((f32[16,8,128]{2,1,0:T(8,128)}), f32[16,8,128]{2,1,0:T(8,128)S(1)}, u32[]{:S(2)}, u32[]{:S(2)}) async-start(f32[16,8,128]{2,1,0:T(8,128)} %broadcast_in_dim.61), calls=%async_computation.6 | async-start | bytes 131072 | tf_op jit(solution)/shard_map/all_to_all | solution.py:23
  188.6 8.8 %collective-permute-start.5 = (bf16[2,128,128]{1,2,0:T(8,128)(2,1)S(1)}, bf16[2,128,128]{1,2,0:T(8,128)(2,1)S(1)}, u32[]{:S(2)}, u32[]{:S(2)}) collective-permute-start(bf16[2,128,128]{1,2,0:T(8,128)(2,1)S(1)} %get-tuple-element.346), channel_id=1, source_target_pairs={{32,0},{64,32},{96,64},{128,96},{160,128},{192,160},{224,192},{256... | collective-permute-start | bytes 196616 | tf_op jit(solution)/shard_map/ppermute | solution.py:18
  194.9 3.2 collective-permute-start.4
  240.0 14.5 %collective-permute-start.7 = (bf16[2,128,128]{1,2,0:T(8,128)(2,1)S(1)}, bf16[2,128,128]{1,2,0:T(8,128)(2,1)S(1)}, u32[]{:S(2)}, u32[]{:S(2)}) collective-permute-start(bf16[2,128,128]{1,2,0:T(8,128)(2,1)S(1)} %get-tuple-element.344), channel_id=1, source_target_pairs={{32,0},{64,32},{96,64},{128,96},{160,128},{192,160},{224,192},{256... | collective-permute-start | bytes 196616 | tf_op jit(solution)/shard_map/ppermute | solution.py:18
  246.5 8.0 %collective-permute-start.6 = (bf16[2,128,128]{1,2,0:T(8,128)(2,1)S(1)}, bf16[2,128,128]{1,2,0:T(8,128)(2,1)S(1)}, u32[]{:S(2)}, u32[]{:S(2)}) collective-permute-start(bf16[2,128,128]{1,2,0:T(8,128)(2,1)S(1)} %get-tuple-element.343), channel_id=1, source_target_pairs={{0,32},{32,64},{64,96},{96,128},{128,160},{160,192},{192,224},{224... | collective-permute-start | bytes 196616 | tf_op jit(solution)/shard_map/ppermute | solution.py:18
  250.7 11.5 %all-to-all-start.15 = ((f32[16,8,128]{2,1,0:T(8,128)}), f32[16,8,128]{2,1,0:T(8,128)S(1)}, u32[]{:S(2)}, u32[]{:S(2)}) async-start(f32[16,8,128]{2,1,0:T(8,128)} %broadcast_in_dim.68), calls=%async_computation.15 | async-start | bytes 131072 | tf_op jit(solution)/shard_map/all_to_all | solution.py:23
  292.8 53.8 %copy-start.18 = (f32[128]{0:T(128)}, f32[128]{0:T(128)S(1)}, u32[]{:S(2)}) copy-start(f32[128]{0:T(128)S(1)} %pad_maximum_fusion.15) | copy-start | bytes 1540
  294.1 14.2 %copy-start.10 = (f32[64]{0:T(128)}, f32[64]{0:T(128)S(1)}, u32[]{:S(2)}) copy-start(f32[64]{0:T(128)S(1)} %get-tuple-element.219) | copy-start | bytes 772
  294.7 51.9 %copy-start.20 = (f32[128]{0:T(128)}, f32[128]{0:T(128)S(1)}, u32[]{:S(2)}) copy-start(f32[128]{0:T(128)S(1)} %pad_maximum_fusion.18) | copy-start | bytes 1540
  308.3 8.8 %collective-permute-start.9 = (bf16[2,128,128]{1,2,0:T(8,128)(2,1)S(1)}, bf16[2,128,128]{1,2,0:T(8,128)(2,1)S(1)}, u32[]{:S(2)}, u32[]{:S(2)}) collective-permute-start(bf16[2,128,128]{1,2,0:T(8,128)(2,1)S(1)} %get-tuple-element.341), channel_id=1, source_target_pairs={{32,0},{64,32},{96,64},{128,96},{160,128},{192,160},{224,192},{256... | collective-permute-start | bytes 196616 | tf_op jit(solution)/shard_map/ppermute | solution.py:18
  314.5 3.2 collective-permute-start.8
  359.9 9.8 %collective-permute-start.11 = (bf16[2,128,128]{1,2,0:T(8,128)(2,1)S(1)}, bf16[2,128,128]{1,2,0:T(8,128)(2,1)S(1)}, u32[]{:S(2)}, u32[]{:S(2)}) collective-permute-start(bf16[2,128,128]{1,2,0:T(8,128)(2,1)S(1)} %get-tuple-element.339), channel_id=1, source_target_pairs={{32,0},{64,32},{96,64},{128,96},{160,128},{192,160},{224,192},{256... | collective-permute-start | bytes 196616 | tf_op jit(solution)/shard_map/ppermute | solution.py:18
  366.1 4.2 collective-permute-start.10
  393.6 8.5 %copy-start.19 = (f32[128]{0:T(128)S(1)}, f32[128]{0:T(128)}, u32[]{:S(2)}) copy-start(f32[128]{0:T(128)} %copy-done.18) | copy-start | bytes 1540
  393.6 8.5 %copy-start.21 = (f32[128]{0:T(128)S(1)}, f32[128]{0:T(128)}, u32[]{:S(2)}) copy-start(f32[128]{0:T(128)} %copy-done.20) | copy-start | bytes 1540
  394.1 35.2 %copy-start.11 = (f32[64]{0:T(128)S(1)}, f32[64]{0:T(128)}, u32[]{:S(2)}) copy-start(f32[64]{0:T(128)} %copy-done.10) | copy-start | bytes 772
  394.1 35.2 %copy-start.12 = (f32[64]{0:T(128)S(1)}, f32[64]{0:T(128)}, u32[]{:S(2)}) copy-start(f32[64]{0:T(128)} %get-tuple-element.217) | copy-start | bytes 772
  394.1 35.2 %copy-start.13 = (f32[64]{0:T(128)S(1)}, f32[64]{0:T(128)}, u32[]{:S(2)}) copy-start(f32[64]{0:T(128)} %get-tuple-element.213) | copy-start | bytes 772
  394.1 35.2 %copy-start.14 = (f32[64]{0:T(128)S(1)}, f32[64]{0:T(128)}, u32[]{:S(2)}) copy-start(f32[64]{0:T(128)} %get-tuple-element.216) | copy-start | bytes 772
  394.1 35.2 %copy-start.15 = (f32[64]{0:T(128)S(1)}, f32[64]{0:T(128)}, u32[]{:S(2)}) copy-start(f32[64]{0:T(128)} %multiply_add_fusion.32) | copy-start | bytes 772
  394.1 35.2 %copy-start.6 = (f32[64]{0:T(128)S(1)}, f32[64]{0:T(128)}, u32[]{:S(2)}) copy-start(f32[64]{0:T(128)} %get-tuple-element.210) | copy-start | bytes 772
  394.1 35.2 %copy-start.7 = (f32[64]{0:T(128)S(1)}, f32[64]{0:T(128)}, u32[]{:S(2)}) copy-start(f32[64]{0:T(128)} %get-tuple-element.208) | copy-start | bytes 772
  394.2 35.2 %copy-start.9 = (f32[64]{0:T(128)S(1)}, f32[64]{0:T(128)}, u32[]{:S(2)}) copy-start(f32[64]{0:T(128)} %get-tuple-element.209) | copy-start | bytes 772
  394.2 35.2 %copy-start.16 = (f32[64]{0:T(128)S(1)}, f32[64]{0:T(128)}, u32[]{:S(2)}) copy-start(f32[64]{0:T(128)} %get-tuple-element.221) | copy-start | bytes 772
  394.2 35.2 %copy-start.17 = (f32[64]{0:T(128)S(1)}, f32[64]{0:T(128)}, u32[]{:S(2)}) copy-start(f32[64]{0:T(128)} %get-tuple-element.207) | copy-start | bytes 772
